TPU v7x, 32 devices: a whole 2x2x4 slice. The times are simulated.
32 devices in a mesh: row: 2 (over y), col: 8 (over z, x), rep: 2 (over core).
Axes of the slice: x: 2, y: 2, z: 4, core: 2. Of those that a mesh axis runs over, the one named last changes fastest.
Arguments:
- gain: float32 [48, 8, 128, 128], P(('row', 'col'), 'rep'), as said below
- coupled_columns: int32 [48, 8], P(('row', 'col')), may hold values from 0 to 47, as said below
- solution: float32 [6144, 512], P(('row', 'col')), may hold values from -6 to 6
- residual: float32 [6144, 512], P(('row', 'col')), may hold values from -6 to 6
- direction: float32 [6144, 512], P(('row', 'col')), may hold values from -6 to 6
Outputs:
- solution_next: float32 [6144, 512], P(('row', 'col'))
- residual_next: float32 [6144, 512], P(('row', 'col'))
- direction_next: float32 [6144, 512], P(('row', 'col'))
Inputs may be any that keep to these rules, and one draw needn't show every extreme that they name: `coupled_columns`: each block row i names first its coupled block columns in ascending order (always i - 1, i, i + 1 where inside 0 to 47, some of i - 3, i - 2, i + 2, i + 3, the coupling being symmetric), at most 7 of them, and then fills the remaining slots with i itself; every named column is within 3 of i. The gain matrix assembled from its blocks is symmetric; padding slots hold zero blocks; each diagonal entry exceeds the sum of the absolute values of the other entries of its row by exactly 1.
All inputs are finite; a program needn't handle non-finite values.
Results may differ from a plain program's by a relative error of at most 0.000061.
Values sent between devices are 32-bit elements; how exact they have to be, the bound alone decides.
A program may use at most 64 MiB of HBM per device.

v0:
```python
import jax
import jax.numpy as jnp
from jax import lax
from jax.sharding import PartitionSpec as P

BLK = 128
reach_blocks = 3


def extended_2(block, sides, width):
    for axis, dim in sides:
        count = lax.axis_size(axis)
        forward = [(i, i + 1) for i in range(count - 1)]
        backward = [(target, source) for source, target in forward]
        low = lax.ppermute(
            lax.slice_in_dim(block, block.shape[dim] - width, None, axis=dim), axis, forward
        )
        high = lax.ppermute(lax.slice_in_dim(block, 0, width, axis=dim), axis, backward)
        block = jnp.concatenate([low, block, high], axis=dim)
    return block


def per_device(gain, coupled_columns, solution, residual, direction):
    row_blocks = coupled_columns.shape[0]
    snapshots = direction.shape[1]
    first_block = lax.axis_index(("row", "col")) * row_blocks
    extended = extended_2(direction, ((("row", "col"), 0),), reach_blocks * BLK)
    segments = extended.reshape(row_blocks + 2 * reach_blocks, BLK, snapshots)
    half_slots = gain.shape[1]
    own_columns = lax.dynamic_slice_in_dim(
        coupled_columns, lax.axis_index("rep") * half_slots, half_slots, 1
    )
    local_index = own_columns - first_block + reach_blocks
    picked = segments[local_index]
    product = jnp.einsum(
        "rkab,rkbs->ras",
        gain,
        picked,
        precision=lax.Precision.HIGHEST,
        preferred_element_type=jnp.float32,
    )
    image = lax.psum(product.reshape(row_blocks * BLK, snapshots), "rep")
    norm_old, curvature, crossing, image_square = lax.psum(
        (
            jnp.sum(residual * residual, axis=0),
            jnp.sum(direction * image, axis=0),
            jnp.sum(residual * image, axis=0),
            jnp.sum(image * image, axis=0),
        ),
        ("row", "col"),
    )
    step_size = norm_old / curvature
    solution_next = solution + step_size * direction
    residual_next = residual - step_size * image
    norm_new = norm_old - 2.0 * step_size * crossing + step_size * step_size * image_square
    direction_next = residual_next + norm_new / norm_old * direction
    return (solution_next, residual_next, direction_next)


def solution(mesh):
    return jax.shard_map(
        per_device,
        mesh=mesh,
        in_specs=(
            P(("row", "col"), "rep", None, None),
            P(("row", "col"), None),
            P(("row", "col"), None),
            P(("row", "col"), None),
            P(("row", "col"), None),
        ),
        out_specs=(P(("row", "col"), None), P(("row", "col"), None), P(("row", "col"), None)),
        check_vma=False,
    )
```

profile of v0, /device:TPU:0, one launch (start us, length us, event | category | flops | bytes accessed | tf_op | source)
XLA Modules:
  0.0 132.4 jit_solution(13395826707546090617)
XLA Ops:
  7.2 0.0 copy-start
  7.2 0.0 all-reduce.3.cloned.1.call-start
  7.2 1.4 %collective-permute-start.1 = (f32[384,512]{1,0:T(8,128)}, f32[384,512]{1,0:T(8,128)S(1)}, u32[]{:S(2)}, u32[]{:S(2)}) collective-permute-start(f32[384,512]{1,0:T(8,128)} %param.9), channel_id=1, source_target_pairs={{2,0},{4,2},{6,4},{8,6},{10,8},{12,10},{14,12},{16,14},{18,16},{20... | collective-permute-start | bytes 2359304 | tf_op jit(solution)/shard_map/ppermute | solution.py:18
  8.7 6.4 %collective-permute-start = (f32[384,512]{1,0:T(8,128)}, f32[384,512]{1,0:T(8,128)}, u32[]{:S(2)}, u32[]{:S(2)}) collective-permute-start(f32[384,512]{1,0:T(8,128)} %param.9), channel_id=1, source_target_pairs={{0,2},{2,4},{4,6},{6,8},{8,10},{10,12},{12,14},{14,16},{16,18},{18... | collective-permute-start | bytes 2359304 | tf_op jit(solution)/shard_map/ppermute | solution.py:15
  15.0 0.8 compare_select_fusion
  15.8 0.1 reshape.18
  15.9 30.9 %collective-permute-done.1 = f32[384,512]{1,0:T(8,128)S(1)} collective-permute-done((f32[384,512]{1,0:T(8,128)}, f32[384,512]{1,0:T(8,128)S(1)}, u32[]{:S(2)}, u32[]{:S(2)}) %collective-permute-start.1) | collective-permute-done | bytes 786464 | tf_op jit(solution)/shard_map/ppermute | solution.py:18
  46.8 0.0 copy-start.4
  46.8 0.9 copy-done.4
  47.7 0.0 collective-permute-done
  47.7 1.8 %pad_maximum_fusion = f32[1152,512]{1,0:T(8,128)S(1)} fusion(f32[384,512]{1,0:T(8,128)} %copy-done.4, f32[384,512]{1,0:T(8,128)} %param.9, f32[384,512]{1,0:T(8,128)} %collective-permute-done), kind=kLoop, calls=%fused_computation.1 | loop fusion | flops 1179648 | bytes 4718592 | tf_op jit(solution)/shard_map/concatenate | solution.py:19
  49.5 2.4 %gather_fusion = f32[12,128,512]{2,1,0:T(8,128)} fusion(f32[9,128,512]{2,1,0:T(8,128)S(1)} %bitcast.10, s32[1024]{0:T(1024)S(1)} %pad_clamp_fusion), kind=kCustom, calls=%fused_computation | custom fusion | bytes 6291504 | tf_op jit(solution)/shard_map/gather | solution.py:34
  51.9 0.0 copy-start.1
  51.9 0.0 copy-start.2
  51.9 0.0 copy-done
  52.0 0.0 copy-start.3
  52.0 4.8 %fusion = f32[3,512,128,1]{1,2,3,0:T(8,128)} fusion(f32[3,4,128,512]{3,2,1,0:T(8,128)} %bitcast.11, f32[3,4,128,128]{3,2,1,0:T(8,128)S(1)} %copy-done), kind=kOutput, calls=%fused_computation.12 | convolution fusion | flops 1207959552 | bytes 4718592 | tf_op jit(solution)/shard_map/rkab,rkbs->ras/dot_general | solution.py:35
  56.7 0.0 all-reduce.3.cloned.1.call-update
  56.7 22.1 %all-reduce.3.cloned.1.call-done = f32[384,512]{1,0:T(8,128)} async-done(((f32[384,512]{1,0:T(8,128)}), f32[384,512]{1,0:T(8,128)}) %all-reduce.3.cloned.1.call-update) | async-done | bytes 786448 | tf_op jit(solution)/shard_map/psum | solution.py:42
  78.8 0.0 copy-done.1
  78.8 0.0 copy-done.2
  78.8 1.4 %multiply_reduce_fusion.1 = (f32[512]{0:T(512)S(1)}, f32[512]{0:T(512)S(1)}, f32[512]{0:T(512)S(1)}, f32[512]{0:T(512)S(1)}) fusion(f32[384,512]{1,0:T(8,128)S(1)} %copy-done.2, f32[384,512]{1,0:T(8,128)} %all-reduce.3.cloned.1.call-done, f32[384,512]{1,0:T(8,128)S(1)} %copy-done.1), kind=kLoop, calls=%fused_computation.4 | loop fusion | flops 1570816 | bytes 2367488 | tf_op jit(solution)/shard_map/reduce_sum | solution.py:47
  80.2 42.5 %all-reduce = (f32[512]{0:T(512)S(1)}, f32[512]{0:T(512)S(1)}, f32[512]{0:T(512)S(1)}, f32[512]{0:T(512)S(1)}) all-reduce(f32[512]{0:T(512)S(1)} %get-tuple-element.6, f32[512]{0:T(512)S(1)} %get-tuple-element.5, f32[512]{0:T(512)S(1)} %get-tuple-element.4, ...), channel_id=1, replica_groups=mesh['row'=2,'col'=8,'rep'=2] {'row','col'}, use_global_device_ids=true, to_apply=%region_1.0 | all-reduce | flops 2048 | bytes 16384 | tf_op jit(solution)/shard_map/psum | solution.py:43
  122.8 0.0 copy-done.3
  122.8 2.8 %multiply_add_fusion = (f32[384,512]{1,0:T(8,128)}, f32[384,512]{1,0:T(8,128)}, f32[384,512]{1,0:T(8,128)}) fusion(f32[384,512]{1,0:T(8,128)S(1)} %copy-done.1, f32[512]{0:T(512)S(1)} %get-tuple-element.13, f32[384,512]{1,0:T(8,128)S(1)} %copy-done.2, f32[384,512]{1,0:T(8,128)} %all-reduce.3.cloned.1.call-done, f32[512]{0:T(512)S(1)} %get-tuple-element.14, ...), kind=kLoop, calls=%fused_computation.2 | loop fusion | flops 1179648 | bytes 5509120 | tf_op jit(solution)/shard_map/add | solution.py:56
  (2 shorter events, 0.0 us)
Async XLA Ops:
  7.2 44.8 %copy-start = (f32[3,4,128,128]{3,2,1,0:T(8,128)S(1)}, f32[3,4,128,128]{3,2,1,0:T(8,128)}, u32[]{:S(2)}) copy-start(f32[3,4,128,128]{3,2,1,0:T(8,128)} %param.5) | copy-start | bytes 2359300
  7.2 71.6 %all-reduce.3.cloned.1.call-start = ((), (), s32[]{:S(2)}) async-start(), calls=%async_computation | async-start | bytes 1572864 | tf_op jit(solution)/shard_map/psum | solution.py:42
  7.2 39.6 %collective-permute-start.1 = (f32[384,512]{1,0:T(8,128)}, f32[384,512]{1,0:T(8,128)S(1)}, u32[]{:S(2)}, u32[]{:S(2)}) collective-permute-start(f32[384,512]{1,0:T(8,128)} %param.9), channel_id=1, source_target_pairs={{2,0},{4,2},{6,4},{8,6},{10,8},{12,10},{14,12},{16,14},{18,16},{20... | collective-permute-start | bytes 2359304 | tf_op jit(solution)/shard_map/ppermute | solution.py:18
  8.7 39.1 %collective-permute-start = (f32[384,512]{1,0:T(8,128)}, f32[384,512]{1,0:T(8,128)}, u32[]{:S(2)}, u32[]{:S(2)}) collective-permute-start(f32[384,512]{1,0:T(8,128)} %param.9), channel_id=1, source_target_pairs={{0,2},{2,4},{4,6},{6,8},{8,10},{10,12},{12,14},{14,16},{16,18},{18... | collective-permute-start | bytes 2359304 | tf_op jit(solution)/shard_map/ppermute | solution.py:15
  46.8 0.9 copy-start.4
  51.9 26.9 %copy-start.1 = (f32[384,512]{1,0:T(8,128)S(1)}, f32[384,512]{1,0:T(8,128)}, u32[]{:S(2)}) copy-start(f32[384,512]{1,0:T(8,128)} %param.9) | copy-start | bytes 2359300
  51.9 26.9 %copy-start.2 = (f32[384,512]{1,0:T(8,128)S(1)}, f32[384,512]{1,0:T(8,128)}, u32[]{:S(2)}) copy-start(f32[384,512]{1,0:T(8,128)} %param.8) | copy-start | bytes 2359300
  52.0 70.8 %copy-start.3 = (f32[384,512]{1,0:T(8,128)S(1)}, f32[384,512]{1,0:T(8,128)}, u32[]{:S(2)}) copy-start(f32[384,512]{1,0:T(8,128)} %param.7) | copy-start | bytes 2359300
Sparse Core Ops, SparseCore 0:
  56.9 21.8 all-reduce.2
where the time goes:
time: 133 us; the launch traced here: 132 us
  waiting for transfers between devices  53 us (40%)
  blocking collectives  42.5 us (32%)
  between operations  14.1 us (11%)
  starting transfers between devices  7.85 us (6%)
  other arithmetic  6.84 us (5%)
  matrix products  4.76 us (4%)
  local copies, waits for them, and re-layouts  3.4 us (3%)
    psum x1, blocking collectives, per_device(): lax.psum((jnp.sum(residual * residual, axis=0), jnp.sum(direction * image...  42.5 us
    ppermute x1, waiting for transfers between devices, extended_2(): lax.ppermute(lax.slice_in_dim(block, 0, width, axis=dim), axis, backward)  30.9 us
    psum x1, waiting for transfers between devices, per_device(): image = lax.psum(product.reshape(row_blocks * BLK, snapshots), 'rep')  22.1 us
    ppermute x1, starting transfers between devices, extended_2(): lax.ppermute(lax.slice_in_dim(block, block.shape[dim] - width, None, axis...  6.39 us
    dot_general x1, matrix products, per_device(): jnp.einsum('rkab,rkbs->ras', gain, picked, precision=lax.Precision.HIGHES...  4.76 us
    add x1, other arithmetic, per_device(): direction_next = residual_next + norm_new / norm_old * direction  2.82 us
  transfers between devices with their start and end apart: 3, of which 2 were waited for; matrix products, arithmetic and copies ran while one was open for 1% of the time, Pallas kernels for 0%

commit v1 on v0

--- a/solution.py
+++ b/solution.py
@@ -5,6 +5,10 @@
 
 BLK = 128
 reach_blocks = 3
+
+
+def _mark_desk(mat):
+    return jnp.sum(jax.lax.all_gather(mat, axis_name="rep"), axis=0)
 
 
 def extended_2(block, sides, width):
@@ -39,7 +43,7 @@
         precision=lax.Precision.HIGHEST,
         preferred_element_type=jnp.float32,
     )
-    image = lax.psum(product.reshape(row_blocks * BLK, snapshots), "rep")
+    image = _mark_desk(product.reshape(row_blocks * BLK, snapshots))
     norm_old, curvature, crossing, image_square = lax.psum(
         (
             jnp.sum(residual * residual, axis=0),

time: 133 us -> 124 us (0.932)
  waiting for transfers between devices: 53 us -> 43.8 us
    psum x1 -> x0, waiting for transfers between devices: 22.1 us -> none  [per_device(): image = lax.psum(product.reshape(row_blocks * BLK, snapshots), 'rep')]
    all_gather x0 -> x1, waiting for transfers between devices: none -> 12.9 us  [_mark_desk(): return jnp.sum(jax.lax.all_gather(mat, axis_name='rep'), axis=0)]
    reduce_sum x0 -> x1, other arithmetic: none -> 1.62 us  [_mark_desk(): return jnp.sum(jax.lax.all_gather(mat, axis_name='rep'), axis=0)]
where the time goes in v1:
time: 124 us
  waiting for transfers between devices  43.8 us (35%)
  blocking collectives  42.5 us (34%)
  between operations  14.1 us (11%)
  starting transfers between devices  7.85 us (6%)
  other arithmetic  7.33 us (6%)
  matrix products  4.61 us (4%)
  local copies, waits for them, and re-layouts  3.4 us (3%)
    psum x1, blocking collectives, per_device(): lax.psum((jnp.sum(residual * residual, axis=0), jnp.sum(direction * image...  42.5 us
    ppermute x1, waiting for transfers between devices, extended_2(): lax.ppermute(lax.slice_in_dim(block, 0, width, axis=dim), axis, backward)  30.9 us
    all_gather x1, waiting for transfers between devices, _mark_desk(): return jnp.sum(jax.lax.all_gather(mat, axis_name='rep'), axis=0)  12.9 us
    ppermute x1, starting transfers between devices, extended_2(): lax.ppermute(lax.slice_in_dim(block, block.shape[dim] - width, None, axis...  6.39 us
    dot_general x1, matrix products, per_device(): jnp.einsum('rkab,rkbs->ras', gain, picked, precision=lax.Precision.HIGHES...  4.61 us
    add x1, other arithmetic, per_device(): direction_next = residual_next + norm_new / norm_old * direction  2.81 us
  transfers between devices with their start and end apart: 3, of which 2 were waited for; matrix products, arithmetic and copies ran while one was open for 1% of the time, Pallas kernels for 0%

profile of v1, /device:TPU:0, one launch (start us, length us, event | category | flops | bytes accessed | tf_op | source)
XLA Modules:
  0.0 123.6 jit_solution(11384302643800708253)
XLA Ops:
  7.2 0.0 copy-start
  7.2 0.0 all-gather.2.cloned.1.call-start
  7.2 1.4 %collective-permute-start.1 = (f32[384,512]{1,0:T(8,128)}, f32[384,512]{1,0:T(8,128)S(1)}, u32[]{:S(2)}, u32[]{:S(2)}) collective-permute-start(f32[384,512]{1,0:T(8,128)} %param.9), channel_id=1, source_target_pairs={{2,0},{4,2},{6,4},{8,6},{10,8},{12,10},{14,12},{16,14},{18,16},{20... | collective-permute-start | bytes 2359304 | tf_op jit(solution)/shard_map/ppermute | solution.py:22
  8.7 6.4 %collective-permute-start = (f32[384,512]{1,0:T(8,128)}, f32[384,512]{1,0:T(8,128)}, u32[]{:S(2)}, u32[]{:S(2)}) collective-permute-start(f32[384,512]{1,0:T(8,128)} %param.9), channel_id=1, source_target_pairs={{0,2},{2,4},{4,6},{6,8},{8,10},{10,12},{12,14},{14,16},{16,18},{18... | collective-permute-start | bytes 2359304 | tf_op jit(solution)/shard_map/ppermute | solution.py:19
  15.0 0.8 compare_select_fusion
  15.8 0.1 reshape.14
  15.9 30.9 %collective-permute-done.1 = f32[384,512]{1,0:T(8,128)S(1)} collective-permute-done((f32[384,512]{1,0:T(8,128)}, f32[384,512]{1,0:T(8,128)S(1)}, u32[]{:S(2)}, u32[]{:S(2)}) %collective-permute-start.1) | collective-permute-done | bytes 786464 | tf_op jit(solution)/shard_map/ppermute | solution.py:22
  46.8 0.0 copy-start.3
  46.8 0.9 copy-done.3
  47.7 0.0 collective-permute-done
  47.7 1.8 %pad_maximum_fusion = f32[1152,512]{1,0:T(8,128)S(1)} fusion(f32[384,512]{1,0:T(8,128)} %copy-done.3, f32[384,512]{1,0:T(8,128)} %param.9, f32[384,512]{1,0:T(8,128)} %collective-permute-done), kind=kLoop, calls=%fused_computation.1 | loop fusion | flops 1179648 | bytes 4718592 | tf_op jit(solution)/shard_map/concatenate | solution.py:23
  49.5 2.4 %gather_fusion = f32[12,128,512]{2,1,0:T(8,128)} fusion(f32[9,128,512]{2,1,0:T(8,128)S(1)} %bitcast.10, s32[1024]{0:T(1024)S(1)} %pad_clamp_fusion), kind=kCustom, calls=%fused_computation | custom fusion | bytes 6291504 | tf_op jit(solution)/shard_map/gather | solution.py:38
  51.9 0.0 copy-done
  51.9 4.6 %fusion = f32[3,512,128,1]{1,2,3,0:T(8,128)} fusion(f32[3,4,128,512]{3,2,1,0:T(8,128)} %bitcast.11, f32[3,4,128,128]{3,2,1,0:T(8,128)S(1)} %copy-done), kind=kOutput, calls=%fused_computation.12 | convolution fusion | flops 1207959552 | bytes 4718592 | tf_op jit(solution)/shard_map/rkab,rkbs->ras/dot_general | solution.py:39
  56.6 0.0 copy-start.1
  56.6 0.0 copy-start.2
  56.6 0.0 all-gather.2.cloned.1.call-update
  56.6 12.9 %all-gather.2.cloned.1.call-done = f32[2,384,512]{2,1,0:T(8,128)} async-done(((f32[1,384,512]{2,1,0:T(8,128)}), f32[2,384,512]{2,1,0:T(8,128)}) %all-gather.2.cloned.1.call-update) | async-done | bytes 1572880 | tf_op jit(solution)/shard_map/all_gather | solution.py:11
  69.5 1.6 %reduce_sum.46 = f32[384,512]{1,0:T(8,128)S(1)} reduce(f32[2,384,512]{2,1,0:T(8,128)} %all-gather.2.cloned.1.call-done, f32[]{:T(128)} %constant.10.clone.1), dimensions={0}, to_apply=%region_2.0 | reduce | flops 196608 | bytes 2359300 | tf_op jit(solution)/shard_map/reduce_sum | solution.py:11
  71.1 0.0 copy-done.1
  71.1 0.0 copy-done.2
  71.1 0.3 multiply_reduce_fusion.1
  71.4 42.5 %all-reduce = (f32[512]{0:T(512)S(1)}, f32[512]{0:T(512)S(1)}, f32[512]{0:T(512)S(1)}, f32[512]{0:T(512)S(1)}) all-reduce(f32[512]{0:T(512)S(1)} %get-tuple-element.6, f32[512]{0:T(512)S(1)} %get-tuple-element.5, f32[512]{0:T(512)S(1)} %get-tuple-element.4, ...), channel_id=1, replica_groups=mesh['row'=2,'col'=8,'rep'=2] {'row','col'}, use_global_device_ids=true, to_apply=%region_1.0 | all-reduce | flops 2048 | bytes 16384 | tf_op jit(solution)/shard_map/psum | solution.py:47
  113.9 2.8 %multiply_add_fusion = (f32[384,512]{1,0:T(8,128)}, f32[384,512]{1,0:T(8,128)}, f32[384,512]{1,0:T(8,128)}) fusion(f32[384,512]{1,0:T(8,128)S(1)} %copy-done.1, f32[512]{0:T(512)S(1)} %get-tuple-element.13, f32[384,512]{1,0:T(8,128)S(1)} %copy-done.2, f32[384,512]{1,0:T(8,128)S(1)} %reduce_sum.46, f32[512]{0:T(512)S(1)} %get-tuple-element.14, f32[384,512]{1,0:T(8,128)} %param.7), kind=kLoop, calls=%fused_computation.2 | loop fusion | flops 1179648 | bytes 5509120 | tf_op jit(solution)/shard_map/add | solution.py:60
  (2 shorter events, 0.0 us)
Async XLA Ops:
  7.2 44.8 %copy-start = (f32[3,4,128,128]{3,2,1,0:T(8,128)S(1)}, f32[3,4,128,128]{3,2,1,0:T(8,128)}, u32[]{:S(2)}) copy-start(f32[3,4,128,128]{3,2,1,0:T(8,128)} %param.5) | copy-start | bytes 2359300
  7.2 62.3 %all-gather.2.cloned.1.call-start = ((), (), s32[]{:S(2)}) async-start(), calls=%async_computation | async-start | bytes 2359296 | tf_op jit(solution)/shard_map/all_gather | solution.py:11
  7.2 39.6 %collective-permute-start.1 = (f32[384,512]{1,0:T(8,128)}, f32[384,512]{1,0:T(8,128)S(1)}, u32[]{:S(2)}, u32[]{:S(2)}) collective-permute-start(f32[384,512]{1,0:T(8,128)} %param.9), channel_id=1, source_target_pairs={{2,0},{4,2},{6,4},{8,6},{10,8},{12,10},{14,12},{16,14},{18,16},{20... | collective-permute-start | bytes 2359304 | tf_op jit(solution)/shard_map/ppermute | solution.py:22
  8.7 39.1 %collective-permute-start = (f32[384,512]{1,0:T(8,128)}, f32[384,512]{1,0:T(8,128)}, u32[]{:S(2)}, u32[]{:S(2)}) collective-permute-start(f32[384,512]{1,0:T(8,128)} %param.9), channel_id=1, source_target_pairs={{0,2},{2,4},{4,6},{6,8},{8,10},{10,12},{12,14},{14,16},{16,18},{18... | collective-permute-start | bytes 2359304 | tf_op jit(solution)/shard_map/ppermute | solution.py:19
  46.8 0.9 copy-start.3
  56.6 14.5 %copy-start.1 = (f32[384,512]{1,0:T(8,128)S(1)}, f32[384,512]{1,0:T(8,128)}, u32[]{:S(2)}) copy-start(f32[384,512]{1,0:T(8,128)} %param.9) | copy-start | bytes 2359300
  56.6 14.6 %copy-start.2 = (f32[384,512]{1,0:T(8,128)S(1)}, f32[384,512]{1,0:T(8,128)}, u32[]{:S(2)}) copy-start(f32[384,512]{1,0:T(8,128)} %param.8) | copy-start | bytes 2359300
Sparse Core Ops, SparseCore 0:
  56.7 12.7 all-gather.1
